TPU v7x, 16 devices: a whole 2x2x2 slice. The times are simulated.
16 devices in a mesh: vp: 16 (over z, y, x, core).
Axes of the slice: x: 2, y: 2, z: 2, core: 2. Of those that a mesh axis runs over, the one named last changes fastest.
Arguments:
- hidden: bfloat16 [256, 1024], replicated
- ln_weight: bfloat16 [1024], replicated
- ln_bias: bfloat16 [1024], replicated
- embedding: bfloat16 [250880, 1024], P('vp')
- temperature: float32 [], replicated
- cand_ids: int32 [256, 128], replicated
Outputs:
- output 1: float32 [256, 250880], P(None, 'vp')
- output 2: float32 [256, 128], replicated
All inputs are finite; a program needn't handle non-finite values.
Results may differ from a plain program's by a relative error of at most 0.001.
Values sent between devices are 32-bit elements.
A program may use at most 1 GiB of HBM per device.

v0:
```python
import jax
import jax.numpy as jnp
from jax import lax
from jax.sharding import PartitionSpec as P, NamedSharding


def layer_norm(hidden, ln_weight, ln_bias):
    hidden_f32 = hidden.astype(jnp.float32)
    row_mean = jnp.mean(hidden_f32, axis=-1, keepdims=True)
    centered = hidden_f32 - row_mean
    row_var = jnp.mean(centered * centered, axis=-1, keepdims=True)
    scaled = centered * lax.rsqrt(row_var + 1e-5)
    return (scaled * ln_weight.astype(jnp.float32) + ln_bias.astype(jnp.float32)).astype(jnp.bfloat16)


def solution(mesh):
    axis_name = mesh.axis_names[0]

    def per_device(hidden, ln_weight, ln_bias, emb_shard, value_a11, cand_ids):
        normed = layer_norm(hidden, ln_weight, ln_bias)
        shard_logits = lax.dot_general(normed, emb_shard, (((1,), (1,)), ((), ())), preferred_element_type=jnp.float32) / value_a11
        full_logits = lax.all_gather(shard_logits, axis_name, axis=1, tiled=True)
        row_max = jnp.max(full_logits, axis=1, keepdims=True)
        exp_sum = jnp.sum(jnp.exp(full_logits - row_max), axis=1, keepdims=True)
        log_norm = row_max + jnp.log(exp_sum)
        shard_lp = shard_logits - log_norm
        cand_lp = jnp.take_along_axis(full_logits, cand_ids, axis=1) - log_norm
        return shard_lp, cand_lp

    return jax.shard_map(
        per_device,
        mesh=mesh,
        in_specs=(P(), P(), P(), P(axis_name, None), P(), P()),
        out_specs=(P(None, axis_name), P()),
        check_vma=False,
    )
```

profile of v0, /device:TPU:0, one launch (start us, length us, event | category | flops | bytes accessed | tf_op | source)
XLA Modules:
  0.0 1470.1 jit_solution(17614303821399290150)
XLA Ops:
  7.2 0.0 all-gather.2.cloned.1.call-start
  7.9 1.2 convert_reduce_fusion
  9.1 1.3 fusion.2
  10.4 0.7 convert_element_type.13
  11.1 0.7 convert_element_type.14
  11.8 0.0 copy-start.1
  11.8 20.7 %convolution_divide_fusion = f32[256,15680]{0,1:T(8,128)} fusion(bf16[15680,1024]{1,0:T(8,128)(2,1)} %param.9, f32[]{:T(128)S(6)} %copy.8, bf16[256,1024]{1,0:T(8,128)(2,1)} %param.6, f32[1024]{0:T(1024)S(1)} %convert_element_type.14, f32[1024]{0:T(1024)S(1)} %convert_element_type.13, f32[256]{0:T(256)S(1)} %add_rsqrt_fusion, f32[256]{0:T(256)S(1)} %broadcast_multiply_fusion), kind=kOutput, calls=%fused_computation.2 | convolution fusion | flops 8226422784 | bytes 48703492 | tf_op jit(solution)/shard_map/dot_general | solution.py:21
  32.5 0.0 all-gather.2.cloned.1.call-update
  32.5 0.0 copy-done.1
  32.5 0.7 fusion.12
  33.2 865.7 %all-gather.2.cloned.1.call-done = f32[256,250880]{0,1:T(8,128)} async-done(((f32[256,15680]{0,1:T(8,128)}), f32[256,250880]{0,1:T(8,128)}) %all-gather.2.cloned.1.call-update) | async-done | bytes 256901136 | tf_op jit(solution)/shard_map/all_gather | solution.py:22
  898.9 77.6 %reduce_max.9 = f32[256]{0:T(256)S(1)} reduce(f32[256,250880]{0,1:T(8,128)} %all-gather.2.cloned.1.call-done, f32[]{:T(128)} %constant.21.clone.1), dimensions={1}, to_apply=%region_2.0 | reduce | flops 64225024 | bytes 256902144 | tf_op jit(solution)/shard_map/reduce_max | solution.py:23
  976.5 77.6 %exponential_reduce_fusion = f32[256]{0:T(256)S(1)} fusion(f32[256,250880]{0,1:T(8,128)} %all-gather.2.cloned.1.call-done, f32[256]{0:T(256)S(1)} %reduce_max.9), kind=kLoop, calls=%fused_computation.1 | loop fusion | flops 128450304 | bytes 256903168 | tf_op jit(solution)/shard_map/reduce_sum | solution.py:24
  1054.1 0.0 copy-start
  1054.1 11.2 broadcast_subtract_fusion
  1065.3 0.0 copy-done
  1065.3 0.0 copy-start.2
  1065.3 397.2 %gather_fusion = f32[32768]{0:T(1024)S(1)} fusion(f32[256,250880]{0,1:T(8,128)} %all-gather.2.cloned.1.call-done, s32[32768]{0:T(1024)S(1)} %copy-done), kind=kCustom, calls=%fused_computation | custom fusion | bytes 524288 | tf_op jit(solution)/shard_map/jit(take_along_axis)/gather | solution.py:27
  1462.5 0.0 copy-done.2
  1462.5 0.8 fusion.11
  (3 shorter events, 0.0 us)
Async XLA Ops:
  7.2 891.7 %all-gather.2.cloned.1.call-start = ((), (), s32[]{:S(2)}) async-start(), calls=%async_computation | async-start | bytes 272957440 | tf_op jit(solution)/shard_map/all_gather | solution.py:22
  11.8 20.7 %copy-start.1 = (s32[256,128]{1,0:T(8,128)S(1)}, s32[256,128]{1,0:T(8,128)}, u32[]{:S(2)}) copy-start(s32[256,128]{1,0:T(8,128)} %param.11) | copy-start | bytes 393220
  1054.1 11.2 copy-start
  1065.3 397.2 %copy-start.2 = (s32[256,128]{1,0:T(8,128)S(1)}, s32[256,128]{1,0:T(8,128)}, u32[]{:S(2)}) copy-start(s32[256,128]{1,0:T(8,128)} %param.11) | copy-start | bytes 393220
Sparse Core Ops, SparseCore 0:
  32.6 866.2 all-gather.1
where the time goes:
time: 1480 us; the launch traced here: 1470 us
  waiting for transfers between devices  866 us (59%)
  local copies, waits for them, and re-layouts  397 us (27%)
  other arithmetic  172 us (12%)
  matrix products  20.7 us (1%)
    all_gather x1, waiting for transfers between devices, per_device(): full_logits = lax.all_gather(shard_logits, axis_name, axis=1, tiled=True)  866 us
    gather x1, local copies, waits for them, and re-layouts, per_device(): cand_lp = jnp.take_along_axis(full_logits, cand_ids, axis=1) - log_norm  397 us
    reduce_sum x1, other arithmetic, per_device(): exp_sum = jnp.sum(jnp.exp(full_logits - row_max), axis=1, keepdims=True)  77.6 us
    reduce_max x1, other arithmetic, per_device(): row_max = jnp.max(full_logits, axis=1, keepdims=True)  77.6 us
  transfers between devices with their start and end apart: 1, of which 1 were waited for; matrix products, arithmetic and copies ran while one was open for 0% of the time, Pallas kernels for 0%

commit v1 on v0

v1 whole, which is shorter than its diff:
```python
import functools

import jax
import jax.numpy as jnp
from jax import lax
from jax.sharding import PartitionSpec as P
from jax.experimental import pallas as pl
from jax.experimental.pallas import tpu as pltpu

N = 16
NV = 15680
D = 1024
B = 256
J = 128
RB = B // N
R = 768
NMAIN = 20
TAIL = NV - NMAIN * R
GX = 2
LOG2E = 1.4426950408889634
MESH = pl.DeviceIdType.MESH


def chunk_list():
    out = [(c * R, R) for c in range(NMAIN)]
    out.append((NMAIN * R, TAIL))
    return out


def lane_gather(x, idx):
    dn = lax.GatherDimensionNumbers(
        offset_dims=(), collapsed_slice_dims=(1,), start_index_map=(1,),
        operand_batching_dims=(0,), start_indices_batching_dims=(0,))
    return lax.gather(x, idx[:, :, None], dn, slice_sizes=(1, 1),
                      mode=lax.GatherScatterMode.PROMISE_IN_BOUNDS)


def local_chunk_stats(z_ref, o, r, k2, m, s):
    u = z_ref[pl.ds(o, r), :].reshape(r // 8, 8, B)
    mn = jnp.maximum(m, jnp.max(u, axis=0))
    p = jnp.exp2((u - mn[None]) * k2[None])
    return mn, s * jnp.exp2((m - mn) * k2) + jnp.sum(p, axis=0)


def local_chunk_gather(z_ref, o, r, loc, acc_ref, scr):
    tiles = [(o + k * 128, o // 128 + k, 0) for k in range(r // 128)]
    if r % 128:
        tiles.append((NV - 128, NV // 128, 128 - NV % 128))
    for ih in range(2):
        for k, (ro, _, _) in enumerate(tiles):
            scr[ih, :, k * 128:(k + 1) * 128] = z_ref[pl.ds(ro, 128), ih * 128:(ih + 1) * 128].T
        for g in range(16):
            r0 = ih * 128 + g * 8
            cv = loc[r0:r0 + 8, :]
            ti = cv >> 7
            li = cv & 127
            acc = acc_ref[r0:r0 + 8, :]
            for k, (_, tid, sh) in enumerate(tiles):
                idx = li if sh == 0 else (li + sh) & 127
                got = lane_gather(scr[ih, g * 8:g * 8 + 8, k * 128:(k + 1) * 128], idx)
                hit = ti == tid
                if sh:
                    hit = hit & (cv < NV)
                acc = jnp.where(hit, got, acc)
            acc_ref[r0:r0 + 8, :] = acc


def stream_kernel(*refs):
    pl.run_scoped(
        functools.partial(stream_body, *refs),
        *[pltpu.ACC(mxu_id=mx)((h, B), jnp.float32) for mx in (0, 1) for h in (R // 2, R // 2, TAIL // 2)])


def stream_body(t_ref, x_hbm, w_ref, b_ref, e_hbm, c_hbm, z_ref, ms_ref, cacc, cbuf,
                ebuf, xbuf, abuf, scr, esem, xsem, csem,
                a00, a01, a0t, a10, a11, a1t):
    me = lax.axis_index("vp")
    chunks = chunk_list()
    accs = [[a00, a01, a0t], [a10, a11, a1t]]

    xcp = pltpu.make_async_copy(x_hbm, xbuf, xsem)
    xcp.start()
    ccp = pltpu.make_async_copy(c_hbm, cbuf, csem)
    ecps = []
    for c, (o, r) in enumerate(chunks):
        cp = pltpu.make_async_copy(e_hbm.at[pl.ds(o, r)], ebuf.at[pl.ds(o, r)], esem.at[c])
        cp.start()
        ecps.append(cp)
        if c == 0:
            ccp.start()

    xcp.wait()
    wv = w_ref[...].astype(jnp.float32)
    bv = b_ref[...].astype(jnp.float32)
    for g in range(0, B, 64):
        x = xbuf[g:g + 64, :].astype(jnp.float32)
        mu = jnp.sum(x, axis=1, keepdims=True) * (1.0 / D)
        xc = x - mu
        var = jnp.sum(xc * xc, axis=1, keepdims=True) * (1.0 / D)
        abuf[g:g + 64, :] = (xc * lax.rsqrt(var + 1e-5) * wv + bv).astype(jnp.bfloat16)

    k2 = (1.0 / t_ref[...]) * LOG2E
    ccp.wait()
    cbuf[...] = cbuf[...] - me * NV
    cacc[...] = jnp.zeros_like(cacc)
    m = jnp.full((8, B), -jnp.inf, jnp.float32)
    s = jnp.zeros((8, B), jnp.float32)

    def issue(c):
        o, r = chunks[c]
        slot = 2 if r == TAIL else c % 2
        h = r // 2
        for kt in range(4):
            for mx in range(2):
                pltpu.matmul_push_rhs(abuf[:, kt * 256:(kt + 1) * 256], staging_register=kt % 2, mxu_index=mx, transpose=True)
            for mx in range(2):
                pltpu.matmul_acc_lhs(accs[mx][slot], ebuf[pl.ds(o + mx * h, h), kt * 256:(kt + 1) * 256], load_staged_rhs=kt % 2)

    def pop(c):
        o, r = chunks[c]
        slot = 2 if r == TAIL else c % 2
        h = r // 2
        for mx in range(2):
            z_ref[pl.ds(o + mx * h, h), :] = pltpu.matmul_pop(accs[mx][slot])

    ns = len(chunks) - GX
    for c in range(len(chunks) + 1):
        if c < len(chunks):
            ecps[c].wait()
            issue(c)
        if c >= 1:
            pop(c - 1)
        if 2 <= c < ns + 2:
            o, r = chunks[c - 2]
            m, s = local_chunk_stats(z_ref, o, r, k2, m, s)
            local_chunk_gather(z_ref, o, r, cbuf, cacc, scr)
    ms_ref[0] = m
    ms_ref[1] = s


def exchange_kernel(t_ref, z_ref, ms_ref, cacc_in, loc, lz_ref, q_ref,
                    scr, cacc, st_send, st_recv, rs_recv, ag_send, ag_recv,
                    st_ss, st_rs, rs_ss, rs_rs, ag_ss, ag_rs):
    me = lax.axis_index("vp")
    peers = [lax.rem(me + k, N) for k in range(1, N)]
    bar = pltpu.get_barrier_semaphore()
    for p in peers:
        pl.semaphore_signal(bar, inc=1, device_id=(p,), device_id_type=MESH)

    inv_t = 1.0 / t_ref[...]
    k2 = inv_t * LOG2E
    chunks = chunk_list()
    ns = len(chunks) - GX
    m, s = ms_ref[0], ms_ref[1]
    for o, r in chunks[ns:]:
        m, s = local_chunk_stats(z_ref, o, r, k2, m, s)
    mloc = jnp.max(m, axis=0, keepdims=True)
    sloc = jnp.sum(s * jnp.exp2((m - mloc) * k2), axis=0, keepdims=True)
    st_send[0:1, :] = mloc
    st_send[1:2, :] = sloc
    cacc[...] = cacc_in[...]
    for o, r in chunks[ns:]:
        local_chunk_gather(z_ref, o, r, loc, cacc, scr)
    pl.semaphore_wait(bar, N - 1)

    st = []
    for k in range(1, N):
        cp = pltpu.make_async_remote_copy(st_send, st_recv.at[k], st_ss.at[k], st_rs.at[k], device_id=(peers[k - 1],), device_id_type=MESH)
        cp.start()
        st.append(cp)
    rs = []
    for k in range(1, N):
        cp = pltpu.make_async_remote_copy(cacc.at[pl.ds(pl.multiple_of(peers[k - 1] * RB, RB), RB)], rs_recv.at[k], rs_ss.at[k], rs_rs.at[k],
                                          device_id=(peers[k - 1],), device_id_type=MESH)
        cp.start()
        rs.append(cp)
    for cp in st:
        cp.wait()
    mp = [mloc] + [st_recv[k, 0:1, :] for k in range(1, N)]
    sp = [sloc] + [st_recv[k, 1:2, :] for k in range(1, N)]
    mg = functools.reduce(jnp.maximum, mp)
    sg = functools.reduce(jnp.add, [b * jnp.exp2((a - mg) * k2) for a, b in zip(mp, sp)])
    lz = mg * inv_t + jnp.log(sg)
    lz_ref[...] = lz
    for cp in rs:
        cp.wait()
    tot = cacc[pl.ds(pl.multiple_of(me * RB, RB), RB), :]
    for k in range(1, N):
        tot = tot + rs_recv[k]
    ag_send[...] = tot
    ag = []
    for k in range(1, N):
        cp = pltpu.make_async_remote_copy(ag_send, ag_recv.at[pl.ds(pl.multiple_of(me * RB, RB), RB)], ag_ss.at[k], ag_rs.at[k],
                                          device_id=(peers[k - 1],), device_id_type=MESH)
        cp.start()
        ag.append(cp)
    cols = [jnp.broadcast_to(lz[:, ih * 128:(ih + 1) * 128], (128, 128)).T for ih in range(2)]
    for cp in ag:
        cp.wait()
    ag_recv[pl.ds(pl.multiple_of(me * RB, RB), RB), :] = tot
    for ih in range(2):
        q_ref[ih * 128:(ih + 1) * 128, :] = ag_recv[ih * 128:(ih + 1) * 128, :] * inv_t - cols[ih]


def solution(mesh):
    axis_name = mesh.axis_names[0]
    vm = pl.BlockSpec(memory_space=pltpu.VMEM)
    anyspec = pl.BlockSpec(memory_space=pl.ANY)
    nch = NMAIN + 1

    def per_device(hidden, ln_weight, ln_bias, emb_shard, temperature, cand_ids):
        t11 = temperature.reshape(1, 1)
        z, ms, cacc, loc = pl.pallas_call(
            stream_kernel,
            out_shape=[pltpu.VMEM((NV, B), jnp.float32), pltpu.VMEM((2, 8, B), jnp.float32),
                       pltpu.VMEM((B, J), jnp.float32), pltpu.VMEM((B, J), jnp.int32)],
            in_specs=[vm, anyspec, vm, vm, anyspec, anyspec],
            out_specs=[vm] * 4,
            scratch_shapes=[
                pltpu.VMEM((NV, D), jnp.bfloat16),
                pltpu.VMEM((B, D), jnp.bfloat16),
                pltpu.VMEM((B, D), jnp.bfloat16),
                pltpu.VMEM((2, 128, R), jnp.float32),
                pltpu.SemaphoreType.DMA((nch,)),
                pltpu.SemaphoreType.DMA,
                pltpu.SemaphoreType.DMA,
            ],
            compiler_params=pltpu.CompilerParams(vmem_limit_bytes=44 * 1024 * 1024),
        )(t11, hidden, ln_weight.reshape(1, D), ln_bias.reshape(1, D), emb_shard, cand_ids)
        pin = lambda a: pltpu.with_memory_space_constraint(a, pltpu.VMEM)
        lz, q = pl.pallas_call(
            exchange_kernel,
            out_shape=[pltpu.VMEM((1, B), jnp.float32), pltpu.VMEM((B, J), jnp.float32)],
            in_specs=[vm] * 5,
            out_specs=[vm] * 2,
            scratch_shapes=[
                pltpu.VMEM((2, 128, R), jnp.float32),
                pltpu.VMEM((B, J), jnp.float32),
                pltpu.VMEM((2, B), jnp.float32),
                pltpu.VMEM((N, 2, B), jnp.float32),
                pltpu.VMEM((N, RB, J), jnp.float32),
                pltpu.VMEM((RB, J), jnp.float32),
                pltpu.VMEM((B, J), jnp.float32),
                pltpu.SemaphoreType.DMA((N,)),
                pltpu.SemaphoreType.DMA((N,)),
                pltpu.SemaphoreType.DMA((N,)),
                pltpu.SemaphoreType.DMA((N,)),
                pltpu.SemaphoreType.DMA((N,)),
                pltpu.SemaphoreType.DMA((N,)),
            ],
            compiler_params=pltpu.CompilerParams(collective_id=0, has_side_effects=True, vmem_limit_bytes=24 * 1024 * 1024),
        )(t11, pin(z), pin(ms), pin(cacc), pin(loc))
        lp = z * (1.0 / temperature) - lz
        return lp.T, q

    return jax.shard_map(
        per_device,
        mesh=mesh,
        in_specs=(P(), P(), P(), P(axis_name, None), P(), P()),
        out_specs=(P(None, axis_name), P()),
        check_vma=False,
    )
```

time: 1480 us -> 50.8 us (0.03)
  waiting for transfers between devices: 866 us -> 0 us
  local copies, waits for them, and re-layouts: 397 us -> 3.21 us
  other arithmetic: 172 us -> 6.14 us
  Pallas kernels: 0 us -> 39.9 us
  matrix products: 20.7 us -> 0 us
    all_gather x1 -> x0, waiting for transfers between devices: 866 us -> none  [per_device(): full_logits = lax.all_gather(shard_logits, axis_name, axis=1, tiled=True)]
    gather x1 -> x0, local copies, waits for them, and re-layouts: 397 us -> none  [per_device(): cand_lp = jnp.take_along_axis(full_logits, cand_ids, axis=1) - log_norm]
    reduce_sum x3 -> x0, other arithmetic: 80.1 us -> none  [the longest x1 77.6 us: per_device(): exp_sum = jnp.sum(jnp.exp(full_logits - row_max), axis=1, keepdims=True)]
    reduce_max x1 -> x0, other arithmetic: 77.6 us -> none  [per_device(): row_max = jnp.max(full_logits, axis=1, keepdims=True)]
    pallas_call x0 -> x2, Pallas kernels: none -> 39.9 us  [the longest x1 25.5 us: per_device(): pl.pallas_call(stream_kernel, out_shape=[pltpu.VMEM((NV, B), jnp.float32)...]
    dot_general x1 -> x0, matrix products: 20.7 us -> none  [per_device(): lax.dot_general(normed, emb_shard, (((1,), (1,)), ((), ())), preferred_el...]
  transfers between devices with their start and end apart: 1 -> 0, of which waited for: 1 -> 0; matrix products, arithmetic and copies ran while one was open for 0% -> 0% of each run, Pallas kernels for 0% -> 0%
where the time goes in v1:
time: 50.8 us; the launch traced here: 50.6 us
  Pallas kernels  39.9 us (79%)
  other arithmetic  6.14 us (12%)
  local copies, waits for them, and re-layouts  3.21 us (6%)
  between operations  1.34 us (3%)
    pallas_call x1, Pallas kernels, per_device(): pl.pallas_call(stream_kernel, out_shape=[pltpu.VMEM((NV, B), jnp.float32)...  25.5 us
    pallas_call x1, Pallas kernels, per_device(): pl.pallas_call(exchange_kernel, out_shape=[pltpu.VMEM((1, B), jnp.float32...  14.4 us
    transpose x1, other arithmetic, per_device(): return (lp.T, q)  6.14 us
    reshape x1, local copies, waits for them, and re-layouts, per_device(): ln_weight.reshape(1, D)  1.28 us
    reshape x1, local copies, waits for them, and re-layouts, per_device(): ln_bias.reshape(1, D)  1.28 us

profile of v1, /device:TPU:0, one launch (start us, length us, event | category | flops | bytes accessed | tf_op | source)
XLA Modules:
  0.0 50.6 jit_solution(8455338973586187453)
XLA Ops:
  1.3 1.3 %reshape.14.refs_2_ = bf16[1,1024]{1,0:T(2,128)(2,1)} reshape(bf16[1024]{0:T(1024)(128)(2,1)} %param.7) | data formatting | bytes 4096 | tf_op jit(solution)/shard_map/reshape | solution.py:229
  2.6 1.3 %reshape.15.refs_3_ = bf16[1,1024]{1,0:T(2,128)(2,1)} reshape(bf16[1024]{0:T(1024)(128)(2,1)} %param.8) | data formatting | bytes 4096 | tf_op jit(solution)/shard_map/reshape | solution.py:229
  3.9 25.5 %shard_map.77 = (f32[15680,256]{1,0:T(8,128)S(1)}, f32[2,8,256]{2,1,0:T(8,128)S(1)}, f32[256,128]{1,0:T(8,128)S(1)}, s32[256,128]{1,0:T(8,128)S(1)}) custom-call(f32[1,1]{1,0:T(1,128)} %bitcast.4.refs_0_, bf16[256,1024]{1,0:T(8,128)(2,1)} %refs_1_.1, bf16[1,1024]{1,0:T(2,128)(2,1)} %reshape.14.refs_2_, bf16[1,1024]{1,0:T(2,128)(2,1)} %reshape.15.refs_3_, ...), custom_call_target="tpu_custom_call" | custom-call | tf_op jit(solution)/shard_map/pallas_call | solution.py:213
  29.4 14.4 %shard_map.78 = (f32[1,256]{1,0:T(1,128)S(1)}, f32[256,128]{1,0:T(8,128)S(1)}) custom-call(f32[1,1]{1,0:T(1,128)} %bitcast.5.t_ref, f32[15680,256]{1,0:T(8,128)S(1)} %get-tuple-element.8.z_ref, f32[2,8,256]{2,1,0:T(8,128)S(1)} %get-tuple-element.9.ms_ref, f32[256,128]{1,0:T(8,128)S(1)} %get-tuple-element.10.cacc_in, s32[256,128]{1,0:T(8,128)S(1)} %get-tuple-element.11.loc), custom_call_target="tpu_custom_call" | custom-call | tf_op jit(solution)/shard_map/pallas_call | solution.py:231
  43.8 6.1 %subtract_bitcast_fusion = f32[256,15680]{0,1:T(8,128)} fusion(f32[15680,256]{1,0:T(8,128)S(1)} %get-tuple-element.8.z_ref, f32[256]{0:T(256)S(1)} %bitcast.6, f32[]{:T(128)S(6)} %div.3), kind=kLoop, calls=%fused_computation | loop fusion | flops 8028160 | bytes 32113668 | tf_op jit(solution)/shard_map/transpose | solution.py:254
  49.9 0.7 %copy.9 = f32[256,128]{1,0:T(8,128)} copy(f32[256,128]{1,0:T(8,128)S(1)} %get-tuple-element.15) | data formatting | bytes 262144

commit v2 on v0

v2 whole, which is shorter than its diff:
```python
import functools

import jax
import jax.numpy as jnp
from jax import lax
from jax.sharding import PartitionSpec as P
from jax.experimental import pallas as pl
from jax.experimental.pallas import tpu as pltpu

N = 16
NV = 15680
NVP = 15744
D = 1024
B = 256
J = 128
RB = B // N
R = 1024
NMAIN = NV // R
TAIL = NV - NMAIN * R
TAILP = NVP - NMAIN * R
NF = 2
LOG2E = 1.4426950408889634
MESH = pl.DeviceIdType.MESH
NT = (((1,), (1,)), ((), ()))


def lane_gather(x, idx):
    dn = lax.GatherDimensionNumbers(
        offset_dims=(), collapsed_slice_dims=(1,), start_index_map=(1,),
        operand_batching_dims=(0,), start_indices_batching_dims=(0,))
    return lax.gather(x, idx[:, :, None], dn, slice_sizes=(1, 1),
                      mode=lax.GatherScatterMode.PROMISE_IN_BOUNDS)


def reduce_list(f, xs):
    while len(xs) > 1:
        xs = [f(xs[i], xs[i + 1]) if i + 1 < len(xs) else xs[i] for i in range(0, len(xs), 2)]
    return xs[0]


def take_chunk(z_ref, col, tile0, ntiles, masked, k2, m_ref, s_ref, loc_ref, acc_ref):
    for g in range(B // 8):
        rows = slice(g * 8, g * 8 + 8)
        us = [z_ref[rows, pl.ds(col + k * 128, 128)] for k in range(ntiles)]
        loc = loc_ref[rows, :]
        ti = (loc >> 7) - tile0
        li = loc & 127
        acc = acc_ref[rows, :]
        for k, u in enumerate(us):
            acc = jnp.where(ti == k, lane_gather(u, li), acc)
        acc_ref[rows, :] = acc
        if masked:
            lane = lax.broadcasted_iota(jnp.int32, (8, 128), 1)
            us[-1] = jnp.where(lane < NV % 128, us[-1], -jnp.inf)
        m = m_ref[rows, :]
        mn = jnp.maximum(m, reduce_list(jnp.maximum, us))
        ps = [jnp.exp2((u - mn) * k2) for u in us]
        s_ref[rows, :] = s_ref[rows, :] * jnp.exp2((m - mn) * k2) + reduce_list(jnp.add, ps)
        m_ref[rows, :] = mn


def head_kernel(t_ref, x_hbm, w_ref, b_ref, e_hbm, c_hbm, z_ref, lz_ref, q_ref,
                ebuf, xbuf, abuf, loc, m_ref, s_ref, cacc, st_send, st_recv, rs_recv, ag_send, ag_recv,
                esem, xsem, csem, st_ss, st_rs, rs_ss, rs_rs, ag_ss, ag_rs):
    me = lax.axis_index("vp")
    peers = [lax.rem(me + k, N) for k in range(1, N)]

    xcp = pltpu.make_async_copy(x_hbm, xbuf, xsem)
    xcp.start()
    ccp = pltpu.make_async_copy(c_hbm, loc, csem)
    ccp.start()

    def ecp(c):
        o = pl.multiple_of(c * R, R)
        return pltpu.make_async_copy(e_hbm.at[pl.ds(o, R)], ebuf.at[pl.ds(o, R)], esem.at[c])

    tcp = pltpu.make_async_copy(e_hbm.at[pl.ds(NMAIN * R, TAIL)], ebuf.at[pl.ds(NMAIN * R, TAIL)], esem.at[NMAIN])
    for c in range(NF):
        ecp(c).start()

    bar = pltpu.get_barrier_semaphore()
    for p in peers:
        pl.semaphore_signal(bar, inc=1, device_id=(p,), device_id_type=MESH)

    ebuf[NV:NVP, :] = jnp.zeros((NVP - NV, D), jnp.bfloat16)
    m_ref[...] = jnp.full_like(m_ref, -jnp.inf)
    s_ref[...] = jnp.zeros_like(s_ref)
    cacc[...] = jnp.zeros_like(cacc)
    inv_t = 1.0 / t_ref[...]
    k2 = inv_t * LOG2E

    xcp.wait()
    for c in range(NF, NMAIN):
        ecp(c).start()
    tcp.start()

    wv = w_ref[...].astype(jnp.float32).reshape(1, D)
    bv = b_ref[...].astype(jnp.float32).reshape(1, D)
    for g in range(0, B, 64):
        x = xbuf[g:g + 64, :].astype(jnp.float32)
        mu = jnp.sum(x, axis=1, keepdims=True) * (1.0 / D)
        xc = x - mu
        var = jnp.sum(xc * xc, axis=1, keepdims=True) * (1.0 / D)
        abuf[g:g + 64, :] = (xc * lax.rsqrt(var + 1e-5) * wv + bv).astype(jnp.bfloat16)

    ccp.wait()
    lv = loc[...] - me * NV
    loc[...] = jnp.where((lv >= 0) & (lv < NV), lv, -1)

    def mm(c):
        o = pl.multiple_of(c * R, R)
        return lax.dot_general(abuf[...], ebuf[pl.ds(o, R), :], NT, preferred_element_type=jnp.float32)

    ecp(0).wait()
    z_ref[:, 0:R] = mm(0)

    def step(c, carry):
        ecp(c).wait()
        z = mm(c)
        o = pl.multiple_of(c * R, R)
        take_chunk(z_ref, o - R, (c - 1) * (R // 128), R // 128, False, k2, m_ref, s_ref, loc, cacc)
        z_ref[:, pl.ds(o, R)] = z
        return carry

    lax.fori_loop(1, NMAIN, step, 0)
    tcp.wait()
    z = lax.dot_general(abuf[...], ebuf[NMAIN * R:NVP, :], NT, preferred_element_type=jnp.float32)
    take_chunk(z_ref, (NMAIN - 1) * R, (NMAIN - 1) * (R // 128), R // 128, False, k2, m_ref, s_ref, loc, cacc)
    z_ref[:, NMAIN * R:NVP] = z
    take_chunk(z_ref, NMAIN * R, NMAIN * (R // 128), TAILP // 128, True, k2, m_ref, s_ref, loc, cacc)

    mt = m_ref[...].T
    mloc = jnp.max(mt, axis=0, keepdims=True)
    sloc = jnp.sum(s_ref[...].T * jnp.exp2((mt - mloc) * k2), axis=0, keepdims=True)
    st_send[0:1, :] = mloc
    st_send[1:2, :] = sloc
    pl.semaphore_wait(bar, N - 1)

    st = []
    for k in range(1, N):
        cp = pltpu.make_async_remote_copy(st_send, st_recv.at[k], st_ss.at[k], st_rs.at[k], device_id=(peers[k - 1],), device_id_type=MESH)
        cp.start()
        st.append(cp)
    rs = []
    for k in range(1, N):
        cp = pltpu.make_async_remote_copy(cacc.at[pl.ds(pl.multiple_of(peers[k - 1] * RB, RB), RB)], rs_recv.at[k], rs_ss.at[k], rs_rs.at[k],
                                          device_id=(peers[k - 1],), device_id_type=MESH)
        cp.start()
        rs.append(cp)
    for cp in st:
        cp.wait()
    mp = [mloc] + [st_recv[k, 0:1, :] for k in range(1, N)]
    sp = [sloc] + [st_recv[k, 1:2, :] for k in range(1, N)]
    mg = functools.reduce(jnp.maximum, mp)
    sg = functools.reduce(jnp.add, [b * jnp.exp2((a - mg) * k2) for a, b in zip(mp, sp)])
    lz = mg * inv_t + jnp.log(sg)
    lz_ref[...] = lz
    for cp in rs:
        cp.wait()
    tot = cacc[pl.ds(pl.multiple_of(me * RB, RB), RB), :]
    for k in range(1, N):
        tot = tot + rs_recv[k]
    ag_send[...] = tot
    ag = []
    for k in range(1, N):
        cp = pltpu.make_async_remote_copy(ag_send, ag_recv.at[pl.ds(pl.multiple_of(me * RB, RB), RB)], ag_ss.at[k], ag_rs.at[k],
                                          device_id=(peers[k - 1],), device_id_type=MESH)
        cp.start()
        ag.append(cp)
    cols = [jnp.broadcast_to(lz[:, ih * 128:(ih + 1) * 128], (128, 128)).T for ih in range(2)]
    for cp in ag:
        cp.wait()
    ag_recv[pl.ds(pl.multiple_of(me * RB, RB), RB), :] = tot
    for ih in range(2):
        q_ref[ih * 128:(ih + 1) * 128, :] = ag_recv[ih * 128:(ih + 1) * 128, :] * inv_t - cols[ih]


WB = 640
WSLOT = 4


def write_kernel(t_ref, z_ref, lz_ref, q_ref, lp_hbm, q_hbm, buf, sems, qsem):
    qcp = pltpu.make_async_copy(q_ref, q_hbm, qsem)
    qcp.start()
    inv_t = 1.0 / t_ref[...]
    lz = lz_ref[...]
    cps = []
    n = NV // WB
    sizes = [WB] * n + ([NV - n * WB] if NV % WB else [])
    o = 0
    for c, r in enumerate(sizes):
        s = c % WSLOT
        if c >= WSLOT:
            cps[c - WSLOT].wait()
        rp = -(-r // 128) * 128
        zt = z_ref[:, o:o + rp].T
        buf[s, 0:r, :] = zt[0:r, :] * inv_t - lz
        cp = pltpu.make_async_copy(buf.at[s, pl.ds(0, r)], lp_hbm.at[pl.ds(o, r)], sems.at[c])
        cp.start()
        cps.append(cp)
        o += r
    for cp in cps[-WSLOT:]:
        cp.wait()
    qcp.wait()


def solution(mesh):
    axis_name = mesh.axis_names[0]
    vm = pl.BlockSpec(memory_space=pltpu.VMEM)
    anyspec = pl.BlockSpec(memory_space=pl.ANY)

    def per_device(hidden, ln_weight, ln_bias, emb_shard, temperature, cand_ids):
        t11 = temperature.reshape(1, 1)
        z, lz, q = pl.pallas_call(
            head_kernel,
            out_shape=[pltpu.VMEM((B, NVP), jnp.float32), pltpu.VMEM((1, B), jnp.float32), pltpu.VMEM((B, J), jnp.float32)],
            in_specs=[vm, anyspec, vm, vm, anyspec, anyspec],
            out_specs=[vm] * 3,
            scratch_shapes=[
                pltpu.VMEM((NVP, D), jnp.bfloat16),
                pltpu.VMEM((B, D), jnp.bfloat16),
                pltpu.VMEM((B, D), jnp.bfloat16),
                pltpu.VMEM((B, J), jnp.int32),
                pltpu.VMEM((B, 128), jnp.float32),
                pltpu.VMEM((B, 128), jnp.float32),
                pltpu.VMEM((B, J), jnp.float32),
                pltpu.VMEM((2, B), jnp.float32),
                pltpu.VMEM((N, 2, B), jnp.float32),
                pltpu.VMEM((N, RB, J), jnp.float32),
                pltpu.VMEM((RB, J), jnp.float32),
                pltpu.VMEM((B, J), jnp.float32),
                pltpu.SemaphoreType.DMA((NMAIN + 1,)),
                pltpu.SemaphoreType.DMA,
                pltpu.SemaphoreType.DMA,
                pltpu.SemaphoreType.DMA((N,)),
                pltpu.SemaphoreType.DMA((N,)),
                pltpu.SemaphoreType.DMA((N,)),
                pltpu.SemaphoreType.DMA((N,)),
                pltpu.SemaphoreType.DMA((N,)),
                pltpu.SemaphoreType.DMA((N,)),
            ],
            compiler_params=pltpu.CompilerParams(collective_id=0, has_side_effects=True, vmem_limit_bytes=44 * 1024 * 1024),
        )(t11, hidden, ln_weight, ln_bias, emb_shard, cand_ids)
        pin = lambda a: pltpu.with_memory_space_constraint(a, pltpu.VMEM)
        nw = -(-NV // WB)
        lp, qo = pl.pallas_call(
            write_kernel,
            out_shape=[jax.ShapeDtypeStruct((NV, B), jnp.float32), jax.ShapeDtypeStruct((B, J), jnp.float32)],
            in_specs=[vm] * 4,
            out_specs=[anyspec] * 2,
            scratch_shapes=[
                pltpu.VMEM((WSLOT, WB, B), jnp.float32),
                pltpu.SemaphoreType.DMA((nw,)),
                pltpu.SemaphoreType.DMA,
            ],
            compiler_params=pltpu.CompilerParams(vmem_limit_bytes=24 * 1024 * 1024),
        )(t11, pin(z), pin(lz), pin(q))
        return lp.T, qo

    return jax.shard_map(
        per_device,
        mesh=mesh,
        in_specs=(P(), P(), P(), P(axis_name, None), P(), P()),
        out_specs=(P(None, axis_name), P()),
        check_vma=False,
    )
```

time: 1480 us -> 36.7 us (0.02)
  waiting for transfers between devices: 866 us -> 0 us
  local copies, waits for them, and re-layouts: 397 us -> 0 us
  other arithmetic: 172 us -> 0 us
  Pallas kernels: 0 us -> 35.3 us
  matrix products: 20.7 us -> 0 us
    all_gather x1 -> x0, waiting for transfers between devices: 866 us -> none  [per_device(): full_logits = lax.all_gather(shard_logits, axis_name, axis=1, tiled=True)]
    gather x1 -> x0, local copies, waits for them, and re-layouts: 397 us -> none  [per_device(): cand_lp = jnp.take_along_axis(full_logits, cand_ids, axis=1) - log_norm]
    reduce_sum x3 -> x0, other arithmetic: 80.1 us -> none  [the longest x1 77.6 us: per_device(): exp_sum = jnp.sum(jnp.exp(full_logits - row_max), axis=1, keepdims=True)]
    reduce_max x1 -> x0, other arithmetic: 77.6 us -> none  [per_device(): row_max = jnp.max(full_logits, axis=1, keepdims=True)]
    pallas_call x0 -> x2, Pallas kernels: none -> 35.3 us  [the longest x1 27.7 us: per_device(): pl.pallas_call(head_kernel, out_shape=[pltpu.VMEM((B, NVP), jnp.float32),...]
    dot_general x1 -> x0, matrix products: 20.7 us -> none  [per_device(): lax.dot_general(normed, emb_shard, (((1,), (1,)), ((), ())), preferred_el...]
  transfers between devices with their start and end apart: 1 -> 0, of which waited for: 1 -> 0; matrix products, arithmetic and copies ran while one was open for 0% -> 0% of each run, Pallas kernels for 0% -> 0%
where the time goes in v2:
time: 36.7 us; the launch traced here: 36.5 us
  Pallas kernels  35.3 us (96%)
  between operations  1.29 us (4%)
    pallas_call x1, Pallas kernels, per_device(): pl.pallas_call(head_kernel, out_shape=[pltpu.VMEM((B, NVP), jnp.float32),...  27.7 us
    pallas_call x1, Pallas kernels, per_device(): pl.pallas_call(write_kernel, out_shape=[jax.ShapeDtypeStruct((NV, B), jnp...  7.59 us

profile of v2, /device:TPU:0, one launch (start us, length us, event | category | flops | bytes accessed | tf_op | source)
XLA Modules:
  0.0 36.5 jit_solution(17955008665940968728)
XLA Ops:
  1.3 27.7 %shard_map.77 = (f32[256,15744]{1,0:T(8,128)S(1)}, f32[1,256]{1,0:T(1,128)S(1)}, f32[256,128]{1,0:T(8,128)S(1)}) custom-call(f32[1,1]{1,0:T(1,128)} %bitcast.2.t_ref, bf16[256,1024]{1,0:T(8,128)(2,1)} %x_hbm.1, bf16[1024]{0:T(1024)(128)(2,1)} %w_ref.1, bf16[1024]{0:T(1024)(128)(2,1)} %b_ref.1, bf16[15680,1024]{1,0:T(8,128)(2,1)} %e_hbm.1, s32[256,128]{1,0:T(8,128)} %c_hbm.1), custom_call_target="tpu_custom_call" | custom-call | tf_op jit(solution)/shard_map/pallas_call | solution.py:214
  29.0 7.6 %shard_map.78 = (f32[15680,256]{1,0:T(8,128)}, f32[256,128]{1,0:T(8,128)}) custom-call(f32[1,1]{1,0:T(1,128)} %bitcast.3.t_ref, f32[256,15744]{1,0:T(8,128)S(1)} %get-tuple-element.7.z_ref, f32[1,256]{1,0:T(1,128)S(1)} %get-tuple-element.8.lz_ref, f32[256,128]{1,0:T(8,128)S(1)} %get-tuple-element.9.q_ref), custom_call_target="tpu_custom_call" | custom-call | tf_op jit(solution)/shard_map/pallas_call | solution.py:246

commit v3 on v2

--- a/solution.py
+++ b/solution.py
@@ -38,10 +38,10 @@
     return xs[0]
 
 
-def take_chunk(z_ref, col, tile0, ntiles, masked, k2, m_ref, s_ref, loc_ref, acc_ref):
+def take_chunk(z_ref, tile0, ntiles, masked, k2, m_ref, s_ref, loc_ref, acc_ref):
     for g in range(B // 8):
         rows = slice(g * 8, g * 8 + 8)
-        us = [z_ref[rows, pl.ds(col + k * 128, 128)] for k in range(ntiles)]
+        us = [z_ref[rows, k * 128:(k + 1) * 128] for k in range(ntiles)]
         loc = loc_ref[rows, :]
         ti = (loc >> 7) - tile0
         li = loc & 127
@@ -60,7 +60,7 @@
 
 
 def head_kernel(t_ref, x_hbm, w_ref, b_ref, e_hbm, c_hbm, z_ref, lz_ref, q_ref,
-                ebuf, xbuf, abuf, loc, m_ref, s_ref, cacc, st_send, st_recv, rs_recv, ag_send, ag_recv,
+                ebuf, xbuf, abuf, zs, loc, m_ref, s_ref, cacc, st_send, st_recv, rs_recv, ag_send, ag_recv,
                 esem, xsem, csem, st_ss, st_rs, rs_ss, rs_rs, ag_ss, ag_rs):
     me = lax.axis_index("vp")
     peers = [lax.rem(me + k, N) for k in range(1, N)]
@@ -111,23 +111,32 @@
         o = pl.multiple_of(c * R, R)
         return lax.dot_general(abuf[...], ebuf[pl.ds(o, R), :], NT, preferred_element_type=jnp.float32)
 
+    def take(slot, c):
+        take_chunk(zs.at[slot], c * (R // 128), R // 128, False, k2, m_ref, s_ref, loc, cacc)
+
+    def put(slot, c, z):
+        zs[slot] = z
+        z_ref[:, pl.ds(pl.multiple_of(c * R, R), R)] = z
+
     ecp(0).wait()
-    z_ref[:, 0:R] = mm(0)
-
-    def step(c, carry):
-        ecp(c).wait()
-        z = mm(c)
-        o = pl.multiple_of(c * R, R)
-        take_chunk(z_ref, o - R, (c - 1) * (R // 128), R // 128, False, k2, m_ref, s_ref, loc, cacc)
-        z_ref[:, pl.ds(o, R)] = z
+    put(0, 0, mm(0))
+
+    def step(i, carry):
+        for d in range(2):
+            c = 1 + 2 * i + d
+            ecp(c).wait()
+            z = mm(c)
+            take(d, c - 1)
+            put(1 - d, c, z)
         return carry
 
-    lax.fori_loop(1, NMAIN, step, 0)
+    lax.fori_loop(0, (NMAIN - 1) // 2, step, 0)
     tcp.wait()
     z = lax.dot_general(abuf[...], ebuf[NMAIN * R:NVP, :], NT, preferred_element_type=jnp.float32)
-    take_chunk(z_ref, (NMAIN - 1) * R, (NMAIN - 1) * (R // 128), R // 128, False, k2, m_ref, s_ref, loc, cacc)
+    take(0, NMAIN - 1)
+    zs[1, :, 0:TAILP] = z
     z_ref[:, NMAIN * R:NVP] = z
-    take_chunk(z_ref, NMAIN * R, NMAIN * (R // 128), TAILP // 128, True, k2, m_ref, s_ref, loc, cacc)
+    take_chunk(zs.at[1], NMAIN * (R // 128), TAILP // 128, True, k2, m_ref, s_ref, loc, cacc)
 
     mt = m_ref[...].T
     mloc = jnp.max(mt, axis=0, keepdims=True)
@@ -176,7 +185,6 @@
 
 
 WB = 640
-WSLOT = 4
 
 
 def write_kernel(t_ref, z_ref, lz_ref, q_ref, lp_hbm, q_hbm, buf, sems, qsem):
@@ -185,21 +193,15 @@
     inv_t = 1.0 / t_ref[...]
     lz = lz_ref[...]
     cps = []
-    n = NV // WB
-    sizes = [WB] * n + ([NV - n * WB] if NV % WB else [])
-    o = 0
-    for c, r in enumerate(sizes):
-        s = c % WSLOT
-        if c >= WSLOT:
-            cps[c - WSLOT].wait()
+    for c, o in enumerate(range(0, NV, WB)):
+        r = min(WB, NV - o)
         rp = -(-r // 128) * 128
         zt = z_ref[:, o:o + rp].T
-        buf[s, 0:r, :] = zt[0:r, :] * inv_t - lz
-        cp = pltpu.make_async_copy(buf.at[s, pl.ds(0, r)], lp_hbm.at[pl.ds(o, r)], sems.at[c])
+        buf[o:o + r, :] = zt[0:r, :] * inv_t - lz
+        cp = pltpu.make_async_copy(buf.at[pl.ds(o, r)], lp_hbm.at[pl.ds(o, r)], sems.at[c])
         cp.start()
         cps.append(cp)
-        o += r
-    for cp in cps[-WSLOT:]:
+    for cp in cps:
         cp.wait()
     qcp.wait()
 
@@ -220,6 +222,7 @@
                 pltpu.VMEM((NVP, D), jnp.bfloat16),
                 pltpu.VMEM((B, D), jnp.bfloat16),
                 pltpu.VMEM((B, D), jnp.bfloat16),
+                pltpu.VMEM((2, B, R), jnp.float32),
                 pltpu.VMEM((B, J), jnp.int32),
                 pltpu.VMEM((B, 128), jnp.float32),
                 pltpu.VMEM((B, 128), jnp.float32),
@@ -249,7 +252,7 @@
             in_specs=[vm] * 4,
             out_specs=[anyspec] * 2,
             scratch_shapes=[
-                pltpu.VMEM((WSLOT, WB, B), jnp.float32),
+                pltpu.VMEM((NV, B), jnp.float32),
                 pltpu.SemaphoreType.DMA((nw,)),
                 pltpu.SemaphoreType.DMA,
             ],

time: 36.7 us -> 34 us (0.926)
  Pallas kernels: 35.3 us -> 32.6 us
    pallas_call x1, Pallas kernels: 7.59 us -> 6.12 us  [per_device(): pl.pallas_call(write_kernel, out_shape=[jax.ShapeDtypeStruct((NV, B), jnp...]
    pallas_call x1, Pallas kernels: 27.7 us -> 26.5 us  [per_device(): pl.pallas_call(head_kernel, out_shape=[pltpu.VMEM((B, NVP), jnp.float32),...]
where the time goes in v3:
time: 34 us; the launch traced here: 33.9 us
  Pallas kernels  32.6 us (96%)
  between operations  1.29 us (4%)
    pallas_call x1, Pallas kernels, per_device(): pl.pallas_call(head_kernel, out_shape=[pltpu.VMEM((B, NVP), jnp.float32),...  26.5 us
    pallas_call x1, Pallas kernels, per_device(): pl.pallas_call(write_kernel, out_shape=[jax.ShapeDtypeStruct((NV, B), jnp...  6.12 us

profile of v3, /device:TPU:0, one launch (start us, length us, event | category | flops | bytes accessed | tf_op | source)
XLA Modules:
  0.0 33.9 jit_solution(10869017562536903355)
XLA Ops:
  1.3 26.5 %shard_map.77 = (f32[256,15744]{1,0:T(8,128)S(1)}, f32[1,256]{1,0:T(1,128)S(1)}, f32[256,128]{1,0:T(8,128)S(1)}) custom-call(f32[1,1]{1,0:T(1,128)} %bitcast.2.t_ref, bf16[256,1024]{1,0:T(8,128)(2,1)} %x_hbm.1, bf16[1024]{0:T(1024)(128)(2,1)} %w_ref.1, bf16[1024]{0:T(1024)(128)(2,1)} %b_ref.1, bf16[15680,1024]{1,0:T(8,128)(2,1)} %e_hbm.1, s32[256,128]{1,0:T(8,128)} %c_hbm.1), custom_call_target="tpu_custom_call" | custom-call | tf_op jit(solution)/shard_map/pallas_call | solution.py:216
  27.7 6.1 %shard_map.78 = (f32[15680,256]{1,0:T(8,128)}, f32[256,128]{1,0:T(8,128)}) custom-call(f32[1,1]{1,0:T(1,128)} %bitcast.3.t_ref, f32[256,15744]{1,0:T(8,128)S(1)} %get-tuple-element.7.z_ref, f32[1,256]{1,0:T(1,128)S(1)} %get-tuple-element.8.lz_ref, f32[256,128]{1,0:T(8,128)S(1)} %get-tuple-element.9.q_ref), custom_call_target="tpu_custom_call" | custom-call | tf_op jit(solution)/shard_map/pallas_call | solution.py:249

commit v4 on v3

--- a/solution.py
+++ b/solution.py
@@ -18,6 +18,7 @@
 NMAIN = NV // R
 TAIL = NV - NMAIN * R
 TAILP = NVP - NMAIN * R
+KS = 512
 NF = 2
 LOG2E = 1.4426950408889634
 MESH = pl.DeviceIdType.MESH
@@ -59,14 +60,18 @@
         m_ref[rows, :] = mn
 
 
-def head_kernel(t_ref, x_hbm, w_ref, b_ref, e_hbm, c_hbm, z_ref, lz_ref, q_ref,
-                ebuf, xbuf, abuf, zs, loc, m_ref, s_ref, cacc, st_send, st_recv, rs_recv, ag_send, ag_recv,
-                esem, xsem, csem, st_ss, st_rs, rs_ss, rs_rs, ag_ss, ag_rs):
+def head_kernel(t_ref, x_hbm, w_hbm, b_hbm, e_hbm, c_hbm, z_ref, lz_ref, q_ref,
+                ebuf, xbuf, w_ref, b_ref, abuf, zs, loc, m_ref, s_ref, cacc, st_send, st_recv, rs_recv, ag_send, ag_recv,
+                esem, xsem, wsem, bsem, csem, st_ss, st_rs, rs_ss, rs_rs, ag_ss, ag_rs):
     me = lax.axis_index("vp")
     peers = [lax.rem(me + k, N) for k in range(1, N)]
 
     xcp = pltpu.make_async_copy(x_hbm, xbuf, xsem)
     xcp.start()
+    wcp = pltpu.make_async_copy(w_hbm, w_ref, wsem)
+    wcp.start()
+    bcp = pltpu.make_async_copy(b_hbm, b_ref, bsem)
+    bcp.start()
     ccp = pltpu.make_async_copy(c_hbm, loc, csem)
     ccp.start()
 
@@ -90,6 +95,8 @@
     k2 = inv_t * LOG2E
 
     xcp.wait()
+    wcp.wait()
+    bcp.wait()
     for c in range(NF, NMAIN):
         ecp(c).start()
     tcp.start()
@@ -107,9 +114,14 @@
     lv = loc[...] - me * NV
     loc[...] = jnp.where((lv >= 0) & (lv < NV), lv, -1)
 
+    def dots(o, r):
+        parts = [lax.dot_general(abuf[:, j:j + KS], ebuf[pl.ds(o, r), j:j + KS], NT, preferred_element_type=jnp.float32)
+                 for j in range(0, D, KS)]
+        return functools.reduce(jnp.add, parts)
+
     def mm(c):
         o = pl.multiple_of(c * R, R)
-        return lax.dot_general(abuf[...], ebuf[pl.ds(o, R), :], NT, preferred_element_type=jnp.float32)
+        return dots(o, R)
 
     def take(slot, c):
         take_chunk(zs.at[slot], c * (R // 128), R // 128, False, k2, m_ref, s_ref, loc, cacc)
@@ -132,7 +144,7 @@
 
     lax.fori_loop(0, (NMAIN - 1) // 2, step, 0)
     tcp.wait()
-    z = lax.dot_general(abuf[...], ebuf[NMAIN * R:NVP, :], NT, preferred_element_type=jnp.float32)
+    z = dots(NMAIN * R, TAILP)
     take(0, NMAIN - 1)
     zs[1, :, 0:TAILP] = z
     z_ref[:, NMAIN * R:NVP] = z
@@ -216,11 +228,13 @@
         z, lz, q = pl.pallas_call(
             head_kernel,
             out_shape=[pltpu.VMEM((B, NVP), jnp.float32), pltpu.VMEM((1, B), jnp.float32), pltpu.VMEM((B, J), jnp.float32)],
-            in_specs=[vm, anyspec, vm, vm, anyspec, anyspec],
+            in_specs=[vm, anyspec, anyspec, anyspec, anyspec, anyspec],
             out_specs=[vm] * 3,
             scratch_shapes=[
                 pltpu.VMEM((NVP, D), jnp.bfloat16),
                 pltpu.VMEM((B, D), jnp.bfloat16),
+                pltpu.VMEM((D,), jnp.bfloat16),
+                pltpu.VMEM((D,), jnp.bfloat16),
                 pltpu.VMEM((B, D), jnp.bfloat16),
                 pltpu.VMEM((2, B, R), jnp.float32),
                 pltpu.VMEM((B, J), jnp.int32),
@@ -233,6 +247,8 @@
                 pltpu.VMEM((RB, J), jnp.float32),
                 pltpu.VMEM((B, J), jnp.float32),
                 pltpu.SemaphoreType.DMA((NMAIN + 1,)),
+                pltpu.SemaphoreType.DMA,
+                pltpu.SemaphoreType.DMA,
                 pltpu.SemaphoreType.DMA,
                 pltpu.SemaphoreType.DMA,
                 pltpu.SemaphoreType.DMA((N,)),

time: 34 us -> 33.3 us (0.979)
  Pallas kernels: 32.6 us -> 31.8 us
    pallas_call x1, Pallas kernels: 26.5 us -> 25.7 us  [per_device(): pl.pallas_call(head_kernel, out_shape=[pltpu.VMEM((B, NVP), jnp.float32),...]
where the time goes in v4:
time: 33.3 us; the launch traced here: 33.1 us
  Pallas kernels  31.8 us (95%)
  between operations  1.29 us (4%)
    pallas_call x1, Pallas kernels, per_device(): pl.pallas_call(head_kernel, out_shape=[pltpu.VMEM((B, NVP), jnp.float32),...  25.7 us
    pallas_call x1, Pallas kernels, per_device(): pl.pallas_call(write_kernel, out_shape=[jax.ShapeDtypeStruct((NV, B), jnp...  6.12 us

profile of v4, /device:TPU:0, one launch (start us, length us, event | category | flops | bytes accessed | tf_op | source)
XLA Modules:
  0.0 33.1 jit_solution(13156545122258313098)
XLA Ops:
  1.3 25.7 %shard_map.77 = (f32[256,15744]{1,0:T(8,128)S(1)}, f32[1,256]{1,0:T(1,128)S(1)}, f32[256,128]{1,0:T(8,128)S(1)}) custom-call(f32[1,1]{1,0:T(1,128)} %bitcast.2.t_ref, bf16[256,1024]{1,0:T(8,128)(2,1)} %x_hbm.1, bf16[1024]{0:T(1024)(128)(2,1)} %w_hbm.1, bf16[1024]{0:T(1024)(128)(2,1)} %b_hbm.1, bf16[15680,1024]{1,0:T(8,128)(2,1)} %e_hbm.1, s32[256,128]{1,0:T(8,128)} %c_hbm.1), custom_call_target="tpu_custom_call" | custom-call | tf_op jit(solution)/shard_map/pallas_call | solution.py:228
  27.0 6.1 %shard_map.78 = (f32[15680,256]{1,0:T(8,128)}, f32[256,128]{1,0:T(8,128)}) custom-call(f32[1,1]{1,0:T(1,128)} %bitcast.3.t_ref, f32[256,15744]{1,0:T(8,128)S(1)} %get-tuple-element.7.z_ref, f32[1,256]{1,0:T(1,128)S(1)} %get-tuple-element.8.lz_ref, f32[256,128]{1,0:T(8,128)S(1)} %get-tuple-element.9.q_ref), custom_call_target="tpu_custom_call" | custom-call | tf_op jit(solution)/shard_map/pallas_call | solution.py:265

commit v5 on v4

--- a/solution.py
+++ b/solution.py
@@ -39,35 +39,43 @@
     return xs[0]
 
 
-def take_chunk(z_ref, tile0, ntiles, masked, k2, m_ref, s_ref, loc_ref, acc_ref):
+def take_candidates(us, rows, tile0, loc_ref, acc_ref):
+    loc = loc_ref[rows, :]
+    ti = (loc >> 7) - tile0
+    li = loc & 127
+    acc = acc_ref[rows, :]
+    for k, u in enumerate(us):
+        acc = jnp.where(ti == k, lane_gather(u, li), acc)
+    acc_ref[rows, :] = acc
+
+
+def take_stats(us, rows, masked, k2, m_ref, s_ref):
+    if masked:
+        lane = lax.broadcasted_iota(jnp.int32, (8, 128), 1)
+        us = us[:-1] + [jnp.where(lane < NV % 128, us[-1], -jnp.inf)]
+    m = m_ref[rows, :]
+    mn = jnp.maximum(m, reduce_list(jnp.maximum, us))
+    ps = [jnp.exp2((u - mn) * k2) for u in us]
+    s_ref[rows, :] = s_ref[rows, :] * jnp.exp2((m - mn) * k2) + reduce_list(jnp.add, ps)
+    m_ref[rows, :] = mn
+
+
+def row_groups(z_ref, ntiles):
     for g in range(B // 8):
         rows = slice(g * 8, g * 8 + 8)
-        us = [z_ref[rows, k * 128:(k + 1) * 128] for k in range(ntiles)]
-        loc = loc_ref[rows, :]
-        ti = (loc >> 7) - tile0
-        li = loc & 127
-        acc = acc_ref[rows, :]
-        for k, u in enumerate(us):
-            acc = jnp.where(ti == k, lane_gather(u, li), acc)
-        acc_ref[rows, :] = acc
-        if masked:
-            lane = lax.broadcasted_iota(jnp.int32, (8, 128), 1)
-            us[-1] = jnp.where(lane < NV % 128, us[-1], -jnp.inf)
-        m = m_ref[rows, :]
-        mn = jnp.maximum(m, reduce_list(jnp.maximum, us))
-        ps = [jnp.exp2((u - mn) * k2) for u in us]
-        s_ref[rows, :] = s_ref[rows, :] * jnp.exp2((m - mn) * k2) + reduce_list(jnp.add, ps)
-        m_ref[rows, :] = mn
-
-
-def head_kernel(t_ref, x_hbm, w_hbm, b_hbm, e_hbm, c_hbm, z_ref, lz_ref, q_ref,
-                ebuf, xbuf, w_ref, b_ref, abuf, zs, loc, m_ref, s_ref, cacc, st_send, st_recv, rs_recv, ag_send, ag_recv,
-                esem, xsem, wsem, bsem, csem, st_ss, st_rs, rs_ss, rs_rs, ag_ss, ag_rs):
+        yield rows, [z_ref[rows, k * 128:(k + 1) * 128] for k in range(ntiles)]
+
+
+def head_kernel(t_hbm, x_hbm, w_hbm, b_hbm, e_hbm, c_hbm, z_ref, lz_ref, q_ref,
+                ebuf, xbuf, t_ref, w_ref, b_ref, abuf, zs, loc, m_ref, s_ref, cacc, st_send, st_recv, rs_recv, ag_send, ag_recv,
+                esem, xsem, tsem, wsem, bsem, csem, st_ss, st_rs, rs_ss, rs_rs, ag_ss, ag_rs):
     me = lax.axis_index("vp")
     peers = [lax.rem(me + k, N) for k in range(1, N)]
 
     xcp = pltpu.make_async_copy(x_hbm, xbuf, xsem)
     xcp.start()
+    tmcp = pltpu.make_async_copy(t_hbm, t_ref, tsem)
+    tmcp.start()
     wcp = pltpu.make_async_copy(w_hbm, w_ref, wsem)
     wcp.start()
     bcp = pltpu.make_async_copy(b_hbm, b_ref, bsem)
@@ -91,9 +99,6 @@
     m_ref[...] = jnp.full_like(m_ref, -jnp.inf)
     s_ref[...] = jnp.zeros_like(s_ref)
     cacc[...] = jnp.zeros_like(cacc)
-    inv_t = 1.0 / t_ref[...]
-    k2 = inv_t * LOG2E
-
     xcp.wait()
     wcp.wait()
     bcp.wait()
@@ -111,6 +116,9 @@
         abuf[g:g + 64, :] = (xc * lax.rsqrt(var + 1e-5) * wv + bv).astype(jnp.bfloat16)
 
     ccp.wait()
+    tmcp.wait()
+    inv_t = 1.0 / t_ref[...]
+    k2 = inv_t * LOG2E
     lv = loc[...] - me * NV
     loc[...] = jnp.where((lv >= 0) & (lv < NV), lv, -1)
 
@@ -124,7 +132,9 @@
         return dots(o, R)
 
     def take(slot, c):
-        take_chunk(zs.at[slot], c * (R // 128), R // 128, False, k2, m_ref, s_ref, loc, cacc)
+        for rows, us in row_groups(zs.at[slot], R // 128):
+            take_candidates(us, rows, c * (R // 128), loc, cacc)
+            take_stats(us, rows, False, k2, m_ref, s_ref)
 
     def put(slot, c, z):
         zs[slot] = z
@@ -145,37 +155,36 @@
     lax.fori_loop(0, (NMAIN - 1) // 2, step, 0)
     tcp.wait()
     z = dots(NMAIN * R, TAILP)
-    take(0, NMAIN - 1)
+    for rows, us in row_groups(zs.at[0], R // 128):
+        take_candidates(us, rows, (NMAIN - 1) * (R // 128), loc, cacc)
     zs[1, :, 0:TAILP] = z
     z_ref[:, NMAIN * R:NVP] = z
-    take_chunk(zs.at[1], NMAIN * (R // 128), TAILP // 128, True, k2, m_ref, s_ref, loc, cacc)
-
-    mt = m_ref[...].T
-    mloc = jnp.max(mt, axis=0, keepdims=True)
-    sloc = jnp.sum(s_ref[...].T * jnp.exp2((mt - mloc) * k2), axis=0, keepdims=True)
-    st_send[0:1, :] = mloc
-    st_send[1:2, :] = sloc
+    for rows, us in row_groups(zs.at[1], TAILP // 128):
+        take_candidates(us, rows, NMAIN * (R // 128), loc, cacc)
     pl.semaphore_wait(bar, N - 1)
 
-    st = []
-    for k in range(1, N):
-        cp = pltpu.make_async_remote_copy(st_send, st_recv.at[k], st_ss.at[k], st_rs.at[k], device_id=(peers[k - 1],), device_id_type=MESH)
-        cp.start()
-        st.append(cp)
     rs = []
     for k in range(1, N):
         cp = pltpu.make_async_remote_copy(cacc.at[pl.ds(pl.multiple_of(peers[k - 1] * RB, RB), RB)], rs_recv.at[k], rs_ss.at[k], rs_rs.at[k],
                                           device_id=(peers[k - 1],), device_id_type=MESH)
         cp.start()
         rs.append(cp)
-    for cp in st:
-        cp.wait()
-    mp = [mloc] + [st_recv[k, 0:1, :] for k in range(1, N)]
-    sp = [sloc] + [st_recv[k, 1:2, :] for k in range(1, N)]
-    mg = functools.reduce(jnp.maximum, mp)
-    sg = functools.reduce(jnp.add, [b * jnp.exp2((a - mg) * k2) for a, b in zip(mp, sp)])
-    lz = mg * inv_t + jnp.log(sg)
-    lz_ref[...] = lz
+
+    for rows, us in row_groups(zs.at[0], R // 128):
+        take_stats(us, rows, False, k2, m_ref, s_ref)
+    for rows, us in row_groups(zs.at[1], TAILP // 128):
+        take_stats(us, rows, True, k2, m_ref, s_ref)
+    mt = m_ref[...].T
+    mloc = jnp.max(mt, axis=0, keepdims=True)
+    sloc = jnp.sum(s_ref[...].T * jnp.exp2((mt - mloc) * k2), axis=0, keepdims=True)
+    st_send[0:1, :] = mloc
+    st_send[1:2, :] = sloc
+    st = []
+    for k in range(1, N):
+        cp = pltpu.make_async_remote_copy(st_send, st_recv.at[k], st_ss.at[k], st_rs.at[k], device_id=(peers[k - 1],), device_id_type=MESH)
+        cp.start()
+        st.append(cp)
+
     for cp in rs:
         cp.wait()
     tot = cacc[pl.ds(pl.multiple_of(me * RB, RB), RB), :]
@@ -188,6 +197,15 @@
                                           device_id=(peers[k - 1],), device_id_type=MESH)
         cp.start()
         ag.append(cp)
+    for cp in st:
+        cp.wait()
+    mp = [mloc] + [st_recv[k, 0:1, :] for k in range(1, N)]
+    sp = [sloc] + [st_recv[k, 1:2, :] for k in range(1, N)]
+    mg = functools.reduce(jnp.maximum, mp)
+    sg = functools.reduce(jnp.add, [b * jnp.exp2((a - mg) * k2) for a, b in zip(mp, sp)])
+    lz = mg * inv_t + jnp.log(sg)
+    lz_ref[0:1, :] = lz
+    lz_ref[1:2, :] = jnp.broadcast_to(inv_t, (1, B))
     cols = [jnp.broadcast_to(lz[:, ih * 128:(ih + 1) * 128], (128, 128)).T for ih in range(2)]
     for cp in ag:
         cp.wait()
@@ -199,11 +217,11 @@
 WB = 640
 
 
-def write_kernel(t_ref, z_ref, lz_ref, q_ref, lp_hbm, q_hbm, buf, sems, qsem):
+def write_kernel(z_ref, lz_ref, q_ref, lp_hbm, q_hbm, buf, sems, qsem):
     qcp = pltpu.make_async_copy(q_ref, q_hbm, qsem)
     qcp.start()
-    inv_t = 1.0 / t_ref[...]
-    lz = lz_ref[...]
+    lz = lz_ref[0:1, :]
+    inv_t = lz_ref[1:2, :]
     cps = []
     for c, o in enumerate(range(0, NV, WB)):
         r = min(WB, NV - o)
@@ -227,12 +245,13 @@
         t11 = temperature.reshape(1, 1)
         z, lz, q = pl.pallas_call(
             head_kernel,
-            out_shape=[pltpu.VMEM((B, NVP), jnp.float32), pltpu.VMEM((1, B), jnp.float32), pltpu.VMEM((B, J), jnp.float32)],
-            in_specs=[vm, anyspec, anyspec, anyspec, anyspec, anyspec],
+            out_shape=[pltpu.VMEM((B, NVP), jnp.float32), pltpu.VMEM((2, B), jnp.float32), pltpu.VMEM((B, J), jnp.float32)],
+            in_specs=[anyspec, anyspec, anyspec, anyspec, anyspec, anyspec],
             out_specs=[vm] * 3,
             scratch_shapes=[
                 pltpu.VMEM((NVP, D), jnp.bfloat16),
                 pltpu.VMEM((B, D), jnp.bfloat16),
+                pltpu.VMEM((1, 1), jnp.float32),
                 pltpu.VMEM((D,), jnp.bfloat16),
                 pltpu.VMEM((D,), jnp.bfloat16),
                 pltpu.VMEM((B, D), jnp.bfloat16),
@@ -251,6 +270,7 @@
                 pltpu.SemaphoreType.DMA,
                 pltpu.SemaphoreType.DMA,
                 pltpu.SemaphoreType.DMA,
+                pltpu.SemaphoreType.DMA,
                 pltpu.SemaphoreType.DMA((N,)),
                 pltpu.SemaphoreType.DMA((N,)),
                 pltpu.SemaphoreType.DMA((N,)),
@@ -265,7 +285,7 @@
         lp, qo = pl.pallas_call(
             write_kernel,
             out_shape=[jax.ShapeDtypeStruct((NV, B), jnp.float32), jax.ShapeDtypeStruct((B, J), jnp.float32)],
-            in_specs=[vm] * 4,
+            in_specs=[vm] * 3,
             out_specs=[anyspec] * 2,
             scratch_shapes=[
                 pltpu.VMEM((NV, B), jnp.float32),
@@ -273,7 +293,7 @@
                 pltpu.SemaphoreType.DMA,
             ],
             compiler_params=pltpu.CompilerParams(vmem_limit_bytes=24 * 1024 * 1024),
-        )(t11, pin(z), pin(lz), pin(q))
+        )(pin(z), pin(lz), pin(q))
         return lp.T, qo
 
     return jax.shard_map(

time: 33.3 us -> 32.9 us (0.988)
  Pallas kernels: 31.8 us -> 31.4 us
    pallas_call x1, Pallas kernels: 25.7 us -> 25.4 us  [per_device(): pl.pallas_call(head_kernel, out_shape=[pltpu.VMEM((B, NVP), jnp.float32),...]
where the time goes in v5:
time: 32.9 us; the launch traced here: 32.7 us
  Pallas kernels  31.4 us (95%)
  between operations  1.29 us (4%)
    pallas_call x1, Pallas kernels, per_device(): pl.pallas_call(head_kernel, out_shape=[pltpu.VMEM((B, NVP), jnp.float32),...  25.4 us
    pallas_call x1, Pallas kernels, per_device(): pl.pallas_call(write_kernel, out_shape=[jax.ShapeDtypeStruct((NV, B), jnp...  6.09 us

profile of v5, /device:TPU:0, one launch (start us, length us, event | category | flops | bytes accessed | tf_op | source)
XLA Modules:
  0.0 32.7 jit_solution(12095216702795220561)
XLA Ops:
  1.3 25.4 %shard_map.77 = (f32[256,15744]{1,0:T(8,128)S(1)}, f32[2,256]{1,0:T(2,128)S(1)}, f32[256,128]{1,0:T(8,128)S(1)}) custom-call(f32[1,1]{1,0:T(1,128)} %bitcast.2.t_hbm, bf16[256,1024]{1,0:T(8,128)(2,1)} %x_hbm.1, bf16[1024]{0:T(1024)(128)(2,1)} %w_hbm.1, bf16[1024]{0:T(1024)(128)(2,1)} %b_hbm.1, bf16[15680,1024]{1,0:T(8,128)(2,1)} %e_hbm.1, s32[256,128]{1,0:T(8,128)} %c_hbm.1), custom_call_target="tpu_custom_call" | custom-call | tf_op jit(solution)/shard_map/pallas_call | solution.py:246
  26.6 6.1 %shard_map.78 = (f32[15680,256]{1,0:T(8,128)}, f32[256,128]{1,0:T(8,128)}) custom-call(f32[256,15744]{1,0:T(8,128)S(1)} %get-tuple-element.7.z_ref, f32[2,256]{1,0:T(2,128)S(1)} %get-tuple-element.8.lz_ref, f32[256,128]{1,0:T(8,128)S(1)} %get-tuple-element.9.q_ref), custom_call_target="tpu_custom_call" | custom-call | tf_op jit(solution)/shard_map/pallas_call | solution.py:285
